TPU v7x, 32 devices: a whole 2x2x4 slice. The times are simulated.
32 devices in a mesh: groups: 2 (over y), aa: 4 (over z), ba: 2 (over x), col: 2 (over core).
Axes of the slice: x: 2, y: 2, z: 4, core: 2. Of those that a mesh axis runs over, the one named last changes fastest.
Arguments:
- hidden: bfloat16 [32, 128, 8192], P(('groups', 'aa'), None, ('ba', 'col')), parts along dimension 0, may hold values from -6 to 6
- key_value_weight: bfloat16 [2048, 8192], P('aa', ('ba', 'col')), may hold values from -0.09375 to 0.09375
- adapter_down_weight: bfloat16 [32, 32, 8192], P(('groups', 'aa'), None, ('ba', 'col')), parts along dimension 0, may hold values from -0.0625 to 0.0625
- adapter_up_weight: bfloat16 [32, 16, 2048], P(('groups', 'aa'), None, ('ba', 'col')), parts along dimension 0, may hold values from -1.5 to 1.5
- prompt_block_count: int32 [16], P('groups'), parts along dimension 0, may hold values from 1 to 3, 16 in all
- request_adapter: int32 [16], P('groups'), parts along dimension 0, may hold values from 0 to 15
- adapter_bank_row: int32 [32], P('groups'), parts along dimension 0, may hold values from 0 to 15, each once
Outputs:
- kv_states: bfloat16 [32, 128, 2048], P(('groups', 'aa'), None, ('ba', 'col')), parts along dimension 0
There are 2 independent parts, one for each index of `groups`. A program takes and returns all parts, laid end to end along the dimension named above; an argument that names none is the same for every part. Nothing has to cross between parts.
Inputs may be any that keep to these rules, and one draw needn't show every extreme that they name: prompt_block_count sum to 16; some request has exactly 3 blocks. `adapter_bank_row`: each bank row holds one adapter; bank row s lies on index s // 4 of aa.
All inputs are finite; a program needn't handle non-finite values.
Results may differ from a plain program's by a relative error of at most 0.001.
Values may be sent and summed in bfloat16 or wider, within the bound.
A program may use at most 128 MiB of HBM per device.

v0:
```python
import jax
import jax.numpy as jnp
from jax import lax
from jax.sharding import PartitionSpec as P


def block_slots(prompt_block_count, request_adapter, adapter_bank_row, block_total):
    block_ids = jnp.arange(block_total, dtype=jnp.int32)
    block_ends = jnp.cumsum(prompt_block_count)
    request_of = jnp.sum((block_ends[None, :] <= block_ids[:, None]).astype(jnp.int32), axis=1)
    request_ids = jnp.arange(prompt_block_count.shape[0], dtype=jnp.int32)
    adapter_of = jnp.sum(
        jnp.where(request_of[:, None] == request_ids[None, :], request_adapter[None, :], 0), axis=1
    )
    adapter_rows = jnp.arange(adapter_bank_row.shape[0], dtype=jnp.int32)
    return jnp.sum(
        jnp.where(adapter_of[:, None] == adapter_rows[None, :], adapter_bank_row[None, :], 0),
        axis=1,
    )


def body(
    hidden,
    key_value_weight,
    adapter_down_weight,
    adapter_up_weight,
    prompt_block_count,
    request_adapter,
    adapter_bank_row,
):
    owners = lax.axis_size("aa")
    owner_index = lax.axis_index("aa")
    shard_count = lax.axis_size(("ba", "col"))
    local_blocks, block_len, feat_width = hidden.shape
    request_grouped, paired_rank, unused_item = adapter_down_weight.shape
    rank_half = paired_rank // 2
    column_span = adapter_up_weight.shape[2]
    bank_row_lookup = block_slots(
        prompt_block_count, request_adapter, adapter_bank_row, local_blocks * owners
    )
    token_rows = hidden.reshape(local_blocks * block_len, feat_width)
    partial_sums = lax.dot_general(
        token_rows,
        lax.all_gather(key_value_weight, "aa", axis=0, tiled=True),
        (((1,), (1,)), ((), ())),
        preferred_element_type=jnp.float32,
    )
    owned = owner_index * request_grouped + jnp.arange(request_grouped, dtype=jnp.int32)
    onehot = (bank_row_lookup[:, None] == owned[None, :]).astype(jnp.bfloat16)
    send_down = jnp.einsum(
        "cn,nrf->crf", onehot, adapter_down_weight, preferred_element_type=jnp.float32
    )
    send_down = send_down.astype(jnp.bfloat16).reshape(
        owners, local_blocks, paired_rank, feat_width
    )
    send_up = jnp.einsum(
        "cn,nrj->crj", onehot, adapter_up_weight, preferred_element_type=jnp.float32
    )
    send_up = send_up.astype(jnp.bfloat16).reshape(owners, local_blocks, rank_half, column_span)
    got_down, got_up = (
        lax.all_to_all(send_down, "aa", split_axis=0, concat_axis=0, tiled=True),
        lax.all_to_all(send_up, "aa", split_axis=0, concat_axis=0, tiled=True),
    )
    down_sel = jnp.sum(got_down, axis=0)
    up_sel = jnp.sum(got_up, axis=0).astype(jnp.float32)
    base_output = lax.psum_scatter(partial_sums, ("ba", "col"), scatter_dimension=1, tiled=True)
    low_part = jnp.einsum("ctf,crf->ctr", hidden, down_sel, preferred_element_type=jnp.float32)
    low_rank = lax.psum(low_part, ("ba", "col"))
    first_col = lax.axis_index(("ba", "col")) * column_span
    active_rank = jnp.where(
        first_col < column_span * shard_count // 2,
        low_rank[:, :, :rank_half],
        low_rank[:, :, rank_half:],
    )
    adapter_output = jnp.einsum(
        "qvy,qyz->qvz", active_rank, up_sel, precision=lax.Precision.HIGHEST
    )
    base_output = base_output.reshape(local_blocks, block_len, column_span)
    return (base_output + adapter_output).astype(jnp.bfloat16)


def solution(mesh):
    placed = (
        P(("groups", "aa"), None, ("ba", "col")),
        P("aa", ("ba", "col")),
        P(("groups", "aa"), None, ("ba", "col")),
        P(("groups", "aa"), None, ("ba", "col")),
        P("groups"),
        P("groups"),
        P("groups"),
    )
    return jax.shard_map(
        body,
        mesh=mesh,
        in_specs=placed,
        out_specs=P(("groups", "aa"), None, ("ba", "col")),
        check_vma=False,
    )
```

profile of v0, /device:TPU:0, one launch (start us, length us, event | category | flops | bytes accessed | tf_op | source)
XLA Modules:
  0.0 268.8 jit_solution(3987146021241611355)
XLA Ops:
  7.4 0.0 copy-start
  7.4 0.0 copy-start.3
  7.4 0.0 copy-start.4
  7.4 0.0 copy-start.5
  7.4 0.0 copy-start.1
  7.4 0.0 all-gather.2.cloned.1.call-start
  7.4 0.7 all-gather.2.cloned.1.call-update
  8.1 0.0 all-reduce.2.cloned.1.call-start
  8.2 0.0 copy-done.3
  8.2 0.2 reduce-window.8
  8.4 0.1 convert_reduce_fusion
  8.5 0.0 copy-done.4
  8.5 0.1 select_reduce_fusion.1
  8.5 0.0 copy-done.5
  8.5 0.2 select_reduce_fusion
  8.7 0.0 copy-done.1
  8.7 2.3 convolution_convert_fusion
  11.0 4.1 %reshape.49 = bf16[4,4,32,2048]{3,1,0,2:T(4,128)(2,1)} reshape(bf16[16,32,2048]{2,0,1:T(8,128)(2,1)} %convolution_convert_fusion) | data formatting | bytes 4194304 | tf_op jit(solution)/shard_map/reshape | solution.py:53
  15.1 2.9 %copy.19 = bf16[4,4,32,2048]{3,1,2,0:T(4,128)(2,1)S(1)} copy(bf16[4,4,32,2048]{3,1,0,2:T(4,128)(2,1)} %reshape.49) | data formatting | bytes 4194304 | tf_op jit(solution)/shard_map/reshape | solution.py:53
  18.0 110.0 %all_to_all.10 = bf16[4,4,32,2048]{3,1,2,0:T(4,128)(2,1)} all-to-all(bf16[4,4,32,2048]{3,1,2,0:T(4,128)(2,1)S(1)} %copy.19), channel_id=1, replica_groups=mesh['groups'=2,'aa'=4,'ba'=2,'col'=2] {'aa'}, dimensions={0} | all-to-all | bytes 4194304 | tf_op jit(solution)/shard_map/all_to_all | solution.py:61
  128.0 3.1 %reduce_sum.54 = bf16[4,32,2048]{2,0,1:T(4,128)(2,1)S(1)} reduce(bf16[4,4,32,2048]{3,1,2,0:T(4,128)(2,1)} %all_to_all.10, bf16[]{:T(256)} %constant.27.clone.1), dimensions={0}, to_apply=%region_5.6 | reduce | flops 786432 | bytes 2621442 | tf_op jit(solution)/shard_map/reduce_sum | solution.py:64
  131.1 0.0 copy-done
  131.2 1.5 convolution_bitcast_fusion
  132.6 0.0 all-reduce.2.cloned.1.call-update
  132.6 0.0 reduce-scatter.2.cloned.1.call-start
  132.7 74.0 %all-gather.2.cloned.1.call-done = bf16[2048,2048]{1,0:T(8,128)(2,1)} async-done(((bf16[512,2048]{1,0:T(8,128)(2,1)}), bf16[2048,2048]{1,0:T(8,128)(2,1)}) %all-gather.2.cloned.1.call-update) | async-done | bytes 8388624 | tf_op jit(solution)/shard_map/all_gather | solution.py:44
  206.7 9.4 %fusion.15 = f32[512,2048]{1,0:T(8,128)} fusion(bf16[512,2048]{1,0:T(8,128)(2,1)S(1)} %bitcast.18, bf16[2048,2048]{1,0:T(8,128)(2,1)} %all-gather.2.cloned.1.call-done), kind=kOutput, calls=%fused_computation.27 | convolution fusion | flops 4294967296 | bytes 14680064 | tf_op jit(solution)/shard_map/dot_general | solution.py:42
  216.1 0.0 copy-start.2
  216.1 0.0 reduce-scatter.2.cloned.1.call-update
  216.2 0.8 copy-done.2
  217.0 0.4 convolution_convert_fusion.1
  217.3 0.1 reshape.50
  217.4 0.8 copy.23
  218.2 3.4 %all-to-all-start.1 = ((bf16[4,4,16,512]{3,1,2,0:T(4,128)(2,1)}), bf16[4,4,16,512]{3,1,2,0:T(4,128)(2,1)S(1)}, u32[]{:S(2)}, u32[]{:S(2)}) async-start(bf16[4,4,16,512]{3,1,2,0:T(4,128)(2,1)} %copy.23), calls=%async_computation.2 | async-start | bytes 524288 | tf_op jit(solution)/shard_map/all_to_all | solution.py:62
  221.6 9.3 %all-to-all-done.1 = bf16[4,4,16,512]{3,1,2,0:T(4,128)(2,1)S(1)} async-done(((bf16[4,4,16,512]{3,1,2,0:T(4,128)(2,1)}), bf16[4,4,16,512]{3,1,2,0:T(4,128)(2,1)S(1)}, u32[]{:S(2)}, u32[]{:S(2)}) %all-to-all-start.1) | async-done | bytes 262176 | tf_op jit(solution)/shard_map/all_to_all | solution.py:62
  230.9 0.1 reduce_sum.55
  231.0 0.0 all-reduce.2.cloned.1.call-done
  231.1 27.6 %reduce-scatter.2.cloned.1.call-done = f32[512,512]{1,0:T(8,128)} async-done(((f32[512,2048]{1,0:T(8,128)}), f32[512,512]{1,0:T(8,128)}) %reduce-scatter.2.cloned.1.call-update) | async-done | bytes 1048592 | tf_op jit(solution)/shard_map/reduce_scatter | solution.py:66
  258.7 2.7 fusion
  (1 shorter events, 0.0 us)
Async XLA Ops:
  7.4 123.8 %copy-start = (bf16[4,128,2048]{2,1,0:T(8,128)(2,1)S(1)}, bf16[4,128,2048]{2,1,0:T(8,128)(2,1)}, u32[]{:S(2)}) copy-start(bf16[4,128,2048]{2,1,0:T(8,128)(2,1)} %param.7) | copy-start | bytes 6291460
  7.4 0.8 copy-start.3
  7.4 1.1 copy-start.4
  7.4 1.2 copy-start.5
  7.4 1.4 copy-start.1
  7.4 199.3 %all-gather.2.cloned.1.call-start = ((), (), s32[]{:S(2)}) async-start(), calls=%async_computation.3 | async-start | bytes 10485760 | tf_op jit(solution)/shard_map/all_gather | solution.py:44
  8.1 223.0 %all-reduce.2.cloned.1.call-start = ((), (), s32[]{:S(2)}) async-start(), calls=%async_computation.5 | async-start | bytes 131072 | tf_op jit(solution)/shard_map/psum | solution.py:68
  132.6 126.1 %reduce-scatter.2.cloned.1.call-start = ((), (), s32[]{:S(2)}) async-start(), calls=%async_computation.4 | async-start | bytes 5242880 | tf_op jit(solution)/shard_map/reduce_scatter | solution.py:66
  216.1 0.8 copy-start.2
  218.2 12.7 %all-to-all-start.1 = ((bf16[4,4,16,512]{3,1,2,0:T(4,128)(2,1)}), bf16[4,4,16,512]{3,1,2,0:T(4,128)(2,1)S(1)}, u32[]{:S(2)}, u32[]{:S(2)}) async-start(bf16[4,4,16,512]{3,1,2,0:T(4,128)(2,1)} %copy.23), calls=%async_computation.2 | async-start | bytes 524288 | tf_op jit(solution)/shard_map/all_to_all | solution.py:62
Sparse Core Ops, SparseCore 0:
  9.8 196.9 all-gather.1
Sparse Core Ops, SparseCore 1:
  132.7 34.8 all-reduce.1
  216.2 42.4 reduce-scatter.1
where the time goes:
time: 269 us
  waiting for transfers between devices  112 us (42%)
  blocking collectives  110 us (41%)
  matrix products  16.2 us (6%)
  between operations  14.9 us (6%)
  local copies, waits for them, and re-layouts  8.71 us (3%)
  other arithmetic  3.8 us (1%)
  starting transfers between devices  3.53 us (1%)
    all_to_all x1, blocking collectives, body(): lax.all_to_all(send_down, 'aa', split_axis=0, concat_axis=0, tiled=True)  110 us
    all_gather x1, waiting for transfers between devices, body(): lax.all_gather(key_value_weight, 'aa', axis=0, tiled=True)  74 us
    reduce_scatter x1, waiting for transfers between devices, body(): lax.psum_scatter(partial_sums, ('ba', 'col'), scatter_dimension=1, tiled=...  27.6 us
    dot_general x1, matrix products, body(): lax.dot_general(token_rows, lax.all_gather(key_value_weight, 'aa', axis=0...  9.41 us
    all_to_all x1, waiting for transfers between devices, body(): lax.all_to_all(send_up, 'aa', split_axis=0, concat_axis=0, tiled=True)  9.28 us
    reshape x2, local copies, waits for them, and re-layouts, body(): send_down.astype(jnp.bfloat16)  7.02 us
  transfers between devices with their start and end apart: 4, of which 3 were waited for; matrix products, arithmetic and copies ran while one was open for 9% of the time, Pallas kernels for 0%

commit v1 on v0

v1 whole, which is shorter than its diff:
```python
import functools

import jax
import jax.numpy as jnp
from jax import lax
from jax.experimental import pallas as pl
from jax.experimental.pallas import tpu as pltpu
from jax.sharding import PartitionSpec as P

MESH = pl.DeviceIdType.MESH
PIECE = 32
NT = (((1,), (1,)), ((), ()))


def block_slots(prompt_block_count, request_adapter, adapter_bank_row, block_total):
    block_ids = jnp.arange(block_total, dtype=jnp.int32)
    block_ends = jnp.cumsum(prompt_block_count)
    request_of = jnp.sum((block_ends[None, :] <= block_ids[:, None]).astype(jnp.int32), axis=1)
    request_ids = jnp.arange(prompt_block_count.shape[0], dtype=jnp.int32)
    adapter_of = jnp.sum(
        jnp.where(request_of[:, None] == request_ids[None, :], request_adapter[None, :], 0), axis=1
    )
    adapter_rows = jnp.arange(adapter_bank_row.shape[0], dtype=jnp.int32)
    return jnp.sum(
        jnp.where(adapter_of[:, None] == adapter_rows[None, :], adapter_bank_row[None, :], 0),
        axis=1,
    )


def kernel(
    dims,
    hid_hbm, w_hbm, down_ref, up_ref, pd_ref, pu_ref,
    out_ref,
    hid, wbuf, sbuf, rbuf, lbuf, fin, lowbuf,
    load_sem, zrecv, yrecv, zsend, ysend, ssend, rrecv, lrecv, lsend, lowsend, lowrecv,
):
    n, groups, cols, shards, blocks, block_len, rank = dims
    chunk, feat = w_hbm.shape
    half = chunk // groups
    piece = min(PIECE, half)
    pieces = half // piece
    span = rbuf.shape[1]
    pair = 2 * rank
    down_rows = blocks * pair
    per_row = feat // span
    me = lax.axis_index("aa")
    group = lax.axis_index("groups")
    shard = lax.axis_index("ba") * cols + lax.axis_index("col")
    has_left, has_right = me > 0, me < n - 1

    def shard_id(j):
        return {"ba": j // cols, "col": j % cols}

    def other_shard(i):
        return lax.rem(shard + i, shards)

    def other_group(i):
        return lax.rem(group + i, groups)

    def remote(src, dst, send, recv, device_id):
        return pltpu.make_async_remote_copy(
            src_ref=src, dst_ref=dst, send_sem=send, recv_sem=recv,
            device_id=device_id, device_id_type=MESH,
        )

    load_w = pltpu.make_async_copy(w_hbm, wbuf.at[me], load_sem.at[0])
    load_h = pltpu.make_async_copy(hid_hbm, hid, load_sem.at[1])
    load_w.start()
    load_h.start()

    barrier = pltpu.get_barrier_semaphore()

    @pl.when(has_left)
    def _():
        pl.semaphore_signal(barrier, inc=1, device_id={"aa": me - 1}, device_id_type=MESH)

    @pl.when(has_right)
    def _():
        pl.semaphore_signal(barrier, inc=1, device_id={"aa": me + 1}, device_id_type=MESH)

    for i in range(1, groups):
        pl.semaphore_signal(
            barrier, inc=1, device_id={"groups": other_group(i)}, device_id_type=MESH
        )
    for i in range(1, shards):
        pl.semaphore_signal(
            barrier, inc=1, device_id=shard_id(other_shard(i)), device_id_type=MESH
        )
    greeted = jnp.where(has_left, 1, 0) + jnp.where(has_right, 1, 0) + groups + shards - 2
    pl.semaphore_wait(barrier, greeted)

    def along(way):
        return {"aa": me + (1 if way == 0 else -1)}

    def lora_copy(way, d):
        return remote(
            lbuf.at[way, d], lbuf.at[way, d], lsend.at[way, d], lrecv.at[way, d], along(way)
        )

    def add_own(d, write):
        tile = min(512, feat)
        for at in range(0, feat, tile):
            own = jnp.dot(
                pd_ref[d], down_ref[:, at:at + tile], preferred_element_type=jnp.float32
            )
            write(slice(0, down_rows), slice(at, at + tile), own)
        own = jnp.dot(pu_ref[d], up_ref[...], preferred_element_type=jnp.float32)
        for c in range(blocks):
            row = down_rows + (c // per_row) * rank
            at = (c % per_row) * span
            write(slice(row, row + rank), slice(at, at + span), own[c * rank:(c + 1) * rank])

    def lora_hop(way, d, valid, has_prev):
        @pl.when(valid)
        def _():
            @pl.when(has_prev)
            def _():
                lora_copy(way, d).wait_recv()

                def write(rows, at, own):
                    lbuf[way, d, rows, at] = (
                        lbuf[way, d, rows, at].astype(jnp.float32) + own
                    ).astype(jnp.bfloat16)

                add_own(d, write)

            @pl.when(jnp.logical_not(has_prev))
            def _():
                def write(rows, at, own):
                    lbuf[way, d, rows, at] = own.astype(jnp.bfloat16)

                add_own(d, write)

            lora_copy(way, d).start()

    def lora(r):
        turn = r - me
        d = n - 1 - turn
        lora_hop(0, d, jnp.logical_and(turn >= 0, d > me), has_left)
        turn = r - (n - 1 - me)
        lora_hop(1, turn, jnp.logical_and(turn >= 0, turn < me), has_right)

    def own_rows(p):
        return pl.ds(pl.multiple_of(group * half + p * piece, piece), piece)

    def z_copy(way, k, p, src=None):
        dst = wbuf.at[k, own_rows(p)]
        return remote(
            dst if src is None else src, dst, zsend.at[way, k], zrecv.at[k, p], along(way)
        )

    def y_copy(i, k, p):
        ref = wbuf.at[k, own_rows(p)]
        return remote(
            ref, ref, ysend.at[k, i], yrecv.at[k, p, i], {"groups": other_group(i)}
        )

    def forward(way, k, p):
        z_copy(way, k, p).wait_recv()

        @pl.when(has_right if way == 0 else has_left)
        def _():
            z_copy(way, k, p).start()

        for i in range(1, groups):
            y_copy(i, k, p).start()

    def product(k, row):
        row = pl.multiple_of(row, piece)
        got = lax.dot_general(
            wbuf[k, pl.ds(row, piece)], hid[...], NT, preferred_element_type=jnp.float32
        )
        column = k * chunk + row
        dest = column // span
        at = pl.ds(pl.multiple_of(column % span, piece), piece)

        @pl.when(dest == shard)
        def _():
            rbuf[shard, at] = got

        @pl.when(dest != shard)
        def _():
            sbuf[dest, at] = got
            remote(
                sbuf.at[dest, at], rbuf.at[shard, at], ssend.at[dest], rrecv.at[shard],
                shard_id(dest),
            ).start()

    def low_copy(i):
        j = other_shard(i)
        return remote(
            lowbuf.at[shard], lowbuf.at[shard], lowsend.at[i], lowrecv.at[shard], shard_id(j)
        )

    def low():
        def write(rows, at, own):
            fin[rows, at] = own.astype(jnp.bfloat16)

        add_own(me, write)
        for way, has_prev in ((0, has_left), (1, has_right)):
            @pl.when(has_prev)
            def _():
                remote(
                    lbuf.at[way, me], lbuf.at[way, me], lsend.at[way, me],
                    lrecv.at[way, me], along(1 - way),
                ).wait_recv()
                fin[...] = (
                    fin[...].astype(jnp.float32) + lbuf[way, me].astype(jnp.float32)
                ).astype(jnp.bfloat16)

        for c in range(blocks):
            lowbuf[shard, c * pair:(c + 1) * pair] = lax.dot_general(
                fin[c * pair:(c + 1) * pair], hid[c * block_len:(c + 1) * block_len], NT,
                preferred_element_type=jnp.float32,
            )
        for i in range(1, shards):
            low_copy(i).start()

    lora(0)
    for p in range(pieces):
        @pl.when(has_right)
        def _():
            z_copy(0, me, p, w_hbm.at[own_rows(p)]).start()

        @pl.when(has_left)
        def _():
            z_copy(1, me, p, w_hbm.at[own_rows(p)]).start()

    load_w.wait()
    load_h.wait()

    def step(s, carry):
        r, p = s // pieces, s % pieces

        @pl.when(jnp.logical_and(s < n * pieces, r > 0))
        def _():
            @pl.when(p == 0)
            def _():
                lora(r)

            @pl.when(s == (n - 1) * pieces)
            def _():
                low()

            @pl.when(me - r >= 0)
            def _():
                forward(0, me - r, p)

            @pl.when(me + r < n)
            def _():
                forward(1, me + r, p)

        @pl.when(s > 0)
        def _():
            r1, p1 = (s - 1) // pieces, (s - 1) % pieces

            def finish(k):
                product(k, group * half + p1 * piece)
                for i in range(1, groups):
                    g = other_group(groups - i)
                    row = g * half + p1 * piece
                    ref = wbuf.at[k, pl.ds(pl.multiple_of(row, piece), piece)]

                    @pl.when(k != me)
                    def _():
                        remote(
                            ref, ref, ysend.at[k, i], yrecv.at[k, p1, i], {"groups": g}
                        ).wait_recv()

                    product(k, row)

            @pl.when(me - r1 >= 0)
            def _():
                finish(me - r1)

            @pl.when(jnp.logical_and(r1 > 0, me + r1 < n))
            def _():
                finish(me + r1)

        return carry

    lax.fori_loop(0, n * pieces + 1, step, 0)

    for i in range(1, shards):
        j = other_shard(i)
        remote(
            lowbuf.at[j], lowbuf.at[j], lowsend.at[i], lowrecv.at[j], shard_id(j)
        ).wait_recv()
    for i in range(1, shards):
        j = other_shard(i)
        remote(rbuf.at[j], rbuf.at[j], ssend.at[j], rrecv.at[j], shard_id(j)).wait_recv()

    keys = shard < shards // 2
    for c in range(blocks):
        total = rbuf[0, :, c * block_len:(c + 1) * block_len]
        low_sum = lowbuf[0, c * pair:(c + 1) * pair]
        for j in range(1, shards):
            total = total + rbuf[j, :, c * block_len:(c + 1) * block_len]
            low_sum = low_sum + lowbuf[j, c * pair:(c + 1) * pair]
        active = jnp.where(keys, low_sum[:rank], low_sum[rank:])
        row = down_rows + (c // per_row) * rank
        at = (c % per_row) * span
        up = fin[row:row + rank, at:at + span].astype(jnp.float32)
        adapted = jnp.dot(
            active.T, up, precision=lax.Precision.HIGHEST, preferred_element_type=jnp.float32
        )
        out_ref[c * block_len:(c + 1) * block_len] = (total.T + adapted).astype(jnp.bfloat16)

    for k in range(n):
        part = wbuf.at[k, pl.ds(0, half)]
        for way, sent in (
            (0, jnp.logical_and(has_right, k <= me)),
            (1, jnp.logical_and(has_left, k >= me)),
        ):
            @pl.when(sent)
            def _():
                remote(
                    part, part, zsend.at[way, k], zrecv.at[k, 0], along(way)
                ).wait_send()

        @pl.when(k != me)
        def _():
            for i in range(1, groups):
                remote(
                    part, part, ysend.at[k, i], yrecv.at[k, 0, i], {"groups": other_group(i)}
                ).wait_send()

        @pl.when(k > me)
        def _():
            lora_copy(0, k).wait_send()

        @pl.when(k < me)
        def _():
            lora_copy(1, k).wait_send()

    for i in range(1, shards):
        j = other_shard(i)
        remote(sbuf.at[j], rbuf.at[shard], ssend.at[j], rrecv.at[shard], shard_id(j)).wait_send()
        low_copy(i).wait_send()


def body(
    sizes,
    hidden,
    key_value_weight,
    adapter_down_weight,
    adapter_up_weight,
    prompt_block_count,
    request_adapter,
    adapter_bank_row,
):
    n, groups, rows_x, cols = sizes
    shards = rows_x * cols
    blocks, block_len, feat = hidden.shape
    bank, pair, _ = adapter_down_weight.shape
    rank = pair // 2
    span = adapter_up_weight.shape[2]
    chunk = key_value_weight.shape[0]
    tokens = blocks * block_len
    half = chunk // groups
    pieces = half // min(PIECE, half)
    slots = block_slots(prompt_block_count, request_adapter, adapter_bank_row, blocks * n)
    owned = lax.axis_index("aa") * bank + jnp.arange(bank, dtype=jnp.int32)
    onehot = slots[:, None] == owned[None, :]

    def picker(width):
        same = jnp.arange(width)[:, None] == jnp.arange(width)[None, :]
        both = jnp.logical_and(onehot[:, None, :, None], same[None, :, None, :])
        return both.astype(jnp.bfloat16).reshape(n, blocks * width, bank * width)

    vmem = pl.BlockSpec(memory_space=pltpu.VMEM)
    hbm = pl.BlockSpec(memory_space=pl.ANY)
    low_rows = blocks * pair + blocks * rank * span // feat
    dma = pltpu.SemaphoreType.DMA
    out = pl.pallas_call(
        functools.partial(kernel, (n, groups, cols, shards, blocks, block_len, rank)),
        out_shape=jax.ShapeDtypeStruct((tokens, span), jnp.bfloat16),
        in_specs=[hbm, hbm, vmem, vmem, vmem, vmem],
        out_specs=vmem,
        scratch_shapes=[
            pltpu.VMEM((tokens, feat), jnp.bfloat16),
            pltpu.VMEM((n, chunk, feat), jnp.bfloat16),
            pltpu.VMEM((shards, span, tokens), jnp.float32),
            pltpu.VMEM((shards, span, tokens), jnp.float32),
            pltpu.VMEM((2, n, low_rows, feat), jnp.bfloat16),
            pltpu.VMEM((low_rows, feat), jnp.bfloat16),
            pltpu.VMEM((shards, blocks * pair, block_len), jnp.float32),
            dma((2,)),
            dma((n, pieces)),
            dma((n, pieces, groups)),
            dma((2, n)),
            dma((n, groups)),
            dma((shards,)),
            dma((shards,)),
            dma((2, n)),
            dma((2, n)),
            dma((shards,)),
            dma((shards,)),
        ],
        compiler_params=pltpu.CompilerParams(
            collective_id=0, has_side_effects=True, vmem_limit_bytes=60 * 1024 * 1024
        ),
    )(
        hidden.reshape(tokens, feat),
        key_value_weight,
        adapter_down_weight.reshape(bank * pair, feat),
        adapter_up_weight.reshape(bank * rank, span),
        picker(pair),
        picker(rank),
    )
    return out.reshape(blocks, block_len, span)


def solution(mesh):
    placed = (
        P(("groups", "aa"), None, ("ba", "col")),
        P("aa", ("ba", "col")),
        P(("groups", "aa"), None, ("ba", "col")),
        P(("groups", "aa"), None, ("ba", "col")),
        P("groups"),
        P("groups"),
        P("groups"),
    )
    sizes = tuple(mesh.shape[axis] for axis in ("aa", "groups", "ba", "col"))
    return jax.shard_map(
        functools.partial(body, sizes),
        mesh=mesh,
        in_specs=placed,
        out_specs=P(("groups", "aa"), None, ("ba", "col")),
        check_vma=False,
    )
```

time: 269 us -> 119 us (0.44)
  waiting for transfers between devices: 112 us -> 0 us
  Pallas kernels: 0 us -> 111 us
  blocking collectives: 110 us -> 0 us
  matrix products: 16.2 us -> 0 us
  between operations: 14.9 us -> 0.04 us
  local copies, waits for them, and re-layouts: 8.71 us -> 3.6 us
  starting transfers between devices: 3.53 us -> 0 us
    pallas_call x0 -> x1, Pallas kernels: none -> 111 us  [body(): pl.pallas_call(functools.partial(kernel, (n, groups, cols, shards, blocks...]
    all_to_all x1 -> x0, blocking collectives: 110 us -> none  [body(): lax.all_to_all(send_down, 'aa', split_axis=0, concat_axis=0, tiled=True)]
    all_gather x1 -> x0, waiting for transfers between devices: 74 us -> none  [body(): lax.all_gather(key_value_weight, 'aa', axis=0, tiled=True)]
    reduce_scatter x1 -> x0, waiting for transfers between devices: 27.6 us -> none  [body(): lax.psum_scatter(partial_sums, ('ba', 'col'), scatter_dimension=1, tiled=...]
    dot_general x5 -> x0, matrix products: 16.2 us -> none  [the longest x1 9.41 us: body(): lax.dot_general(token_rows, lax.all_gather(key_value_weight, 'aa', axis=0...]
    all_to_all x1 -> x0, waiting for transfers between devices: 9.28 us -> none  [body(): lax.all_to_all(send_up, 'aa', split_axis=0, concat_axis=0, tiled=True)]
    reshape x4 -> x0, local copies, waits for them, and re-layouts: 7.88 us -> none  [the longest x2 7.02 us: body(): send_down.astype(jnp.bfloat16)]
    all_to_all x1 -> x0, starting transfers between devices: 3.41 us -> none  [body(): lax.all_to_all(send_up, 'aa', split_axis=0, concat_axis=0, tiled=True)]
  transfers between devices with their start and end apart: 4 -> 0, of which waited for: 3 -> 0; matrix products, arithmetic and copies ran while one was open for 9% -> 0% of each run, Pallas kernels for 0% -> 0%
where the time goes in v1:
time: 119 us; the launch traced here: 118 us
  Pallas kernels  111 us (93%)
  local copies, waits for them, and re-layouts  3.6 us (3%)
  other arithmetic  3.09 us (3%)
    pallas_call x1, Pallas kernels, body(): pl.pallas_call(functools.partial(kernel, (n, groups, cols, shards, blocks...  111 us

profile of v1, /device:TPU:0, one launch (start us, length us, event | category | flops | bytes accessed | tf_op | source)
XLA Modules:
  0.0 117.7 jit_solution(16142167488823871361)
XLA Ops:
  0.0 0.8 reduce-window.8
  0.8 0.1 convert_reduce_fusion
  0.9 0.7 select_reduce_fusion.1
  1.7 0.8 select_reduce_fusion
  2.5 0.1 broadcast_compare_fusion
  2.6 0.2 and_convert_fusion.1
  2.8 0.8 reshape.113.pu_ref
  3.6 0.3 and_convert_fusion
  3.9 0.9 reshape.112.pd_ref
  4.9 111.0 %shard_map.73 = bf16[512,512]{1,0:T(8,128)(2,1)} custom-call(bf16[512,2048]{1,0:T(8,128)(2,1)} %bitcast.6, bf16[512,2048]{1,0:T(8,128)(2,1)} %w_hbm.1, bf16[128,2048]{1,0:T(8,128)(2,1)} %bitcast.8, bf16[64,512]{1,0:T(8,128)(2,1)} %bitcast.9, bf16[4,128,128]{2,1,0:T(8,128)(2,1)} %reshape.112.pd_ref, bf16[4,64,64]{2,1,0:T(8,128)(2,1)} %reshape.113.pu_ref), custom_call_target="tpu_custom_call" | custom-call | tf_op jit(solution)/shard_map/pallas_call | solution.py:375
  115.9 1.9 %copy.9 = bf16[4,128,512]{2,1,0:T(8,128)(2,1)} copy(bf16[4,128,512]{2,1,0:T(8,128)(2,1)} %bitcast.7) | data formatting | bytes 1048576
  (3 shorter events, 0.0 us)

commit v2 on v1

--- a/solution.py
+++ b/solution.py
@@ -250,9 +250,8 @@
             def _():
                 forward(1, me + r, p)
 
-        @pl.when(s > 0)
-        def _():
-            r1, p1 = (s - 1) // pieces, (s - 1) % pieces
+        def compute(at):
+            r1, p1 = at // pieces, at % pieces
 
             def finish(k):
                 product(k, group * half + p1 * piece)
@@ -276,6 +275,26 @@
             @pl.when(jnp.logical_and(r1 > 0, me + r1 < n))
             def _():
                 finish(me + r1)
+
+        late = s - (n - 1) * pieces
+        inner = jnp.logical_and(me > 0, me < n - 1)
+        behind = (n - 2) * pieces + 2 * late
+
+        @pl.when(jnp.logical_and(jnp.logical_not(inner), s > 0))
+        def _():
+            compute(s - 1)
+
+        @pl.when(jnp.logical_and(inner, jnp.logical_and(late < 0, s >= pieces)))
+        def _():
+            compute(s - pieces)
+
+        @pl.when(jnp.logical_and(inner, late > 0))
+        def _():
+            compute(behind - 1)
+
+        @pl.when(jnp.logical_and(inner, jnp.logical_and(late >= 0, late < pieces)))
+        def _():
+            compute(behind)
 
         return carry
 

time: 119 us -> 116 us (0.975)
  the two profiles are of different devices: /device:TPU:0 before, /device:TPU:16 now
where the time goes in v2:
time: 116 us
  Pallas kernels  109 us (94%)
  local copies, waits for them, and re-layouts  3.6 us (3%)
  other arithmetic  3.09 us (3%)
    pallas_call x1, Pallas kernels, body(): pl.pallas_call(functools.partial(kernel, (n, groups, cols, shards, blocks...  109 us

profile of v2, /device:TPU:16, one launch (start us, length us, event | category | flops | bytes accessed | tf_op | source)
XLA Modules:
  0.0 116.2 jit_solution(11352770618432753223)
XLA Ops:
  0.0 0.8 reduce-window.8
  0.8 0.1 convert_reduce_fusion
  0.9 0.7 select_reduce_fusion.1
  1.7 0.8 select_reduce_fusion
  2.5 0.1 broadcast_compare_fusion
  2.6 0.2 and_convert_fusion.1
  2.8 0.8 reshape.113.pu_ref
  3.6 0.3 and_convert_fusion
  3.9 0.9 reshape.112.pd_ref
  4.9 109.4 %shard_map.73 = bf16[512,512]{1,0:T(8,128)(2,1)} custom-call(bf16[512,2048]{1,0:T(8,128)(2,1)} %bitcast.6, bf16[512,2048]{1,0:T(8,128)(2,1)} %w_hbm.1, bf16[128,2048]{1,0:T(8,128)(2,1)} %bitcast.8, bf16[64,512]{1,0:T(8,128)(2,1)} %bitcast.9, bf16[4,128,128]{2,1,0:T(8,128)(2,1)} %reshape.112.pd_ref, bf16[4,64,64]{2,1,0:T(8,128)(2,1)} %reshape.113.pu_ref), custom_call_target="tpu_custom_call" | custom-call | tf_op jit(solution)/shard_map/pallas_call | solution.py:394
  114.3 1.9 %copy.9 = bf16[4,128,512]{2,1,0:T(8,128)(2,1)} copy(bf16[4,128,512]{2,1,0:T(8,128)(2,1)} %bitcast.7) | data formatting | bytes 1048576
  (3 shorter events, 0.0 us)
